TPU v7x, 32 devices: a whole 2x2x4 slice. The times are simulated.
32 devices in a mesh: row: 4 (over y, x), col: 8 (over z, core).
Axes of the slice: x: 2, y: 2, z: 4, core: 2. Of those that a mesh axis runs over, the one named last changes fastest.
Arguments:
- old_residual: float32 [1024, 16384], P(('row', 'col')), may hold values from -6 to 6
- group_map: int32 [32, 4], replicated, may hold values from 0 to 127, as said below
- q_factor: float32 [16384, 32], P('col', 'row'), may hold values from -0.046875 to 0.046875
Outputs:
- relaid: float32 [1024, 16384], P('row', 'col')
- projection: float32 [32, 1024], P(None, ('row', 'col'))
- row_norms: float32 [1024], P(('row', 'col'))
Inputs may be any that keep to these rules, and one draw needn't show every extreme that they name: `group_map`: all entries together are each group id 0 to 127 once; row d (old device d) holds exactly one id of each range k * 32 to (k + 1) * 32 - 1, in any slot order.
All inputs are finite; a program needn't handle non-finite values.
Results may differ from a plain program's by a relative error of at most 0.00007.
Values sent between devices are 32-bit elements; how exact they have to be, the bound alone decides.
A program may use at most 64 MiB of HBM per device.

v0:
```python
import jax
import jax.numpy as jnp
from jax import lax
from jax.sharding import PartitionSpec as P

epsilon = 1e-06


def on_device(old_residual, group_map, q_factor):
    row_count = lax.axis_size("row")
    column_count = lax.axis_size("col")
    devices_all = row_count * column_count
    my_row = lax.axis_index("row")
    my_column = lax.axis_index("col")
    position = my_row * column_count + my_column
    group_rows = old_residual.shape[0] // row_count
    full_width = old_residual.shape[1]
    block_width = full_width // column_count
    own_ids = lax.dynamic_index_in_dim(group_map, position, 0, keepdims=False)
    sending = jnp.argsort(own_ids)
    stored = jnp.take(old_residual.reshape(row_count, group_rows, full_width), sending, axis=0)
    pieces = stored.reshape(row_count, group_rows, column_count, block_width).transpose(0, 2, 1, 3)
    flat_pieces = pieces.reshape(devices_all, group_rows, block_width)
    received = lax.all_to_all(flat_pieces, ("row", "col"), split_axis=0, concat_axis=0, tiled=True)
    sorted_map = jnp.sort(group_map, axis=1)
    arriving_ids = lax.dynamic_index_in_dim(sorted_map, my_row, 1, keepdims=False)
    placement = jnp.argsort(arriving_ids)
    arranged = jnp.take(received, placement, axis=0)
    relaid_block = arranged.reshape(devices_all * group_rows, block_width)
    factor_full = lax.all_gather(q_factor, "row", axis=1, tiled=True)
    projected_share = lax.psum_scatter(
        jnp.dot(
            relaid_block,
            factor_full,
            precision=lax.Precision.HIGHEST,
            preferred_element_type=jnp.float32,
        ),
        "col",
        scatter_dimension=0,
        tiled=True,
    )
    squares = jnp.sum(relaid_block * relaid_block, axis=1)
    square_total = lax.psum_scatter(squares, "col", scatter_dimension=0, tiled=True)
    row_norms = jnp.sqrt(square_total / full_width + epsilon)
    return (relaid_block, projected_share.T, row_norms)


def solution(mesh):
    placed = (P(("row", "col"), None), P(), P("col", "row"))
    return jax.shard_map(
        on_device,
        mesh=mesh,
        in_specs=placed,
        out_specs=(P("row", "col"), P(None, ("row", "col")), P(("row", "col"))),
        check_vma=False,
    )
```

profile of v0, /device:TPU:0, one launch (start us, length us, event | category | flops | bytes accessed | tf_op | source)
XLA Modules:
  0.0 133.8 jit_solution(3552242644922017772)
XLA Ops:
  7.2 0.0 copy-start
  7.2 1.0 dynamic-slice_reduce_fusion
  8.2 0.7 sort.51
  9.0 2.0 %gather_fusion = f32[4,8,16384]{2,1,0:T(8,128)} fusion(f32[4,8,16384]{2,1,0:T(8,128)S(1)} %bitcast.13, s32[1024]{0:T(1024)S(1)} %pad_clamp_fusion.1), kind=kCustom, calls=%fused_computation | custom fusion | bytes 4194320 | tf_op jit(solution)/shard_map/jit(_take)/gather | solution.py:21
  11.0 3.3 %broadcast_select_fusion = f32[4,8,8,2048]{3,1,2,0:T(8,128)} fusion(f32[4,8,8,2048]{3,1,2,0:T(8,128)} %bitcast.15, pred[4]{0:T(512)(128)(4,1)S(1)} %compare_and_fusion), kind=kLoop, calls=%fused_computation.4 | loop fusion | flops 524288 | bytes 4194308 | tf_op jit(solution)/shard_map/jit(_take)/select_n | solution.py:21
  14.3 7.5 %all-to-all-start = ((f32[32,8,2048]{2,1,0:T(8,128)}), f32[32,8,2048]{2,1,0:T(8,128)}, u32[]{:S(2)}, u32[]{:S(2)}) async-start(f32[32,8,2048]{2,1,0:T(8,128)} %bitcast.14), calls=%async_computation | async-start | bytes 4194304 | tf_op jit(solution)/shard_map/all_to_all | solution.py:24
  21.7 0.0 reduce-scatter.2.cloned.1.call-start
  21.8 0.6 dynamic-slice
  23.1 0.6 sort.49
  23.7 1.6 %sort.50 = (s32[32]{0:T(128)}, s32[32]{0:T(128)S(1)}) sort(s32[32]{0:T(128)S(1)} %dynamic-slice_bitcast_fusion, s32[32]{0:T(128)S(1)} %iota.12), dimensions={0}, to_apply=%region_1.2 | sort | flops 160 | bytes 512 | tf_op jit(solution)/shard_map/jit(argsort)/sort | solution.py:27
  25.3 0.1 broadcast_in_dim.32
  25.4 0.1 broadcast_in_dim.33
  25.5 16.7 %all_gather.3 = f32[2048,32]{0,1:T(8,128)S(1)} all-gather(f32[2048,8]{0,1:T(8,128)S(1)} %copy-done.1), channel_id=1, replica_groups=mesh['row'=4,'col'=8] {'row'}, dimensions={1}, use_global_device_ids=true | all-gather | bytes 327680 | tf_op jit(solution)/shard_map/all_gather | solution.py:30
  42.2 29.5 %all-to-all-done = f32[32,8,2048]{2,1,0:T(8,128)} async-done(((f32[32,8,2048]{2,1,0:T(8,128)}), f32[32,8,2048]{2,1,0:T(8,128)}, u32[]{:S(2)}, u32[]{:S(2)}) %all-to-all-start) | async-done | bytes 2097184 | tf_op jit(solution)/shard_map/all_to_all | solution.py:24
  71.7 3.6 %gather_fusion.1 = f32[32,8,2048]{2,1,0:T(8,128)} fusion(f32[32,8,2048]{2,1,0:T(8,128)} %all-to-all-done, s32[1024]{0:T(1024)S(1)} %pad_clamp_fusion), kind=kCustom, calls=%fused_computation.1 | custom fusion | bytes 4194432 | tf_op jit(solution)/shard_map/jit(_take)/gather | solution.py:28
  75.3 1.9 %multiply_reduce_fusion = f32[32,8]{1,0:T(8,128)S(1)} fusion(f32[32,8,2048]{2,1,0:T(8,128)} %gather_fusion.1, pred[32]{0:T(512)(128)(4,1)S(1)} %compare_and_fusion.1), kind=kLoop, calls=%fused_computation.3 | loop fusion | flops 1572608 | bytes 2098208 | tf_op jit(solution)/shard_map/reduce_sum | solution.py:42
  77.2 0.1 reduce_sum.12
  77.3 3.1 %bitcast_select_fusion = f32[256,2048]{1,0:T(8,128)} fusion(f32[32,8,2048]{2,1,0:T(8,128)} %gather_fusion.1, pred[256]{0:T(512)(128)(4,1)S(1)} %broadcast_in_dim.33), kind=kLoop, calls=%fused_computation.2 | loop fusion | flops 524288 | bytes 4194560 | tf_op jit(solution)/shard_map/jit(_take)/select_n | solution.py:28
  80.5 13.6 %all-reduce = f32[256]{0:T(256)S(1)} all-reduce(f32[256]{0:T(256)S(1)} %reduce_sum.12), channel_id=3, replica_groups=mesh['row'=4,'col'=8] {'col'}, use_global_device_ids=true, to_apply=%region_5.6.clone | all-reduce | flops 256 | bytes 2048
  94.0 4.0 %fusion.2 = f32[256,32]{1,0:T(8,128)} fusion(f32[256,2048]{1,0:T(8,128)} %bitcast_select_fusion, f32[2048,32]{0,1:T(8,128)S(1)} %all_gather.3), kind=kOutput, calls=%fused_computation.16 | convolution fusion | flops 201326592 | bytes 2392064 | tf_op jit(solution)/shard_map/dot_general | solution.py:32
  98.0 0.0 reduce-scatter.2.cloned.1.call-update
  98.1 0.6 fusion.1
  98.7 26.9 %reduce-scatter.2.cloned.1.call-done = f32[32,32]{1,0:T(8,128)} async-done(((f32[256,32]{1,0:T(8,128)}), f32[32,32]{1,0:T(8,128)}) %reduce-scatter.2.cloned.1.call-update) | async-done | bytes 4112 | tf_op jit(solution)/shard_map/reduce_scatter | solution.py:31
  125.5 1.4 %copy.8 = f32[32,32]{1,0:T(8,128)} copy(f32[32,32]{0,1:T(8,128)} %bitcast.16) | data formatting | bytes 8192
  (17 shorter events, 0.1 us)
Async XLA Ops:
  7.2 1.8 %copy-start = (f32[32,16384]{1,0:T(8,128)S(1)}, f32[32,16384]{1,0:T(8,128)}, u32[]{:S(2)}) copy-start(f32[32,16384]{1,0:T(8,128)} %param.3) | copy-start | bytes 6291460
  14.3 7.5 %copy-start.3 = (u32[32]{0:T(128)S(1)}, u32[32]{0:T(128)}, u32[]{:S(2)}) copy-start(u32[32]{0:T(128)} %constant.57) | copy-start | bytes 388
  14.3 8.8 %copy-start.2 = (s32[32,4]{0,1:T(4,128)S(1)}, s32[32,4]{0,1:T(4,128)}, u32[]{:S(2)}) copy-start(s32[32,4]{0,1:T(4,128)} %param.4) | copy-start | bytes 1540
  14.3 11.2 %copy-start.1 = (f32[2048,8]{0,1:T(8,128)S(1)}, f32[2048,8]{0,1:T(8,128)}, u32[]{:S(2)}) copy-start(f32[2048,8]{0,1:T(8,128)} %param.5) | copy-start | bytes 196612
  14.3 57.5 %all-to-all-start = ((f32[32,8,2048]{2,1,0:T(8,128)}), f32[32,8,2048]{2,1,0:T(8,128)}, u32[]{:S(2)}, u32[]{:S(2)}) async-start(f32[32,8,2048]{2,1,0:T(8,128)} %bitcast.14), calls=%async_computation | async-start | bytes 4194304 | tf_op jit(solution)/shard_map/all_to_all | solution.py:24
  21.7 103.8 %reduce-scatter.2.cloned.1.call-start = ((), (), s32[]{:S(2)}) async-start(), calls=%async_computation.2 | async-start | bytes 147456 | tf_op jit(solution)/shard_map/reduce_scatter | solution.py:31
Sparse Core Ops, SparseCore 0:
  98.2 27.3 reduce-scatter.1
where the time goes:
time: 134 us
  waiting for transfers between devices  56.4 us (42%)
  blocking collectives  30.3 us (23%)
  between operations  14.8 us (11%)
  other arithmetic  11.9 us (9%)
  local copies, waits for them, and re-layouts  8.86 us (7%)
  starting transfers between devices  7.5 us (6%)
  matrix products  3.99 us (3%)
    all_to_all x1, waiting for transfers between devices, on_device(): lax.all_to_all(flat_pieces, ('row', 'col'), split_axis=0, concat_axis=0,...  29.5 us
    reduce_scatter x1, waiting for transfers between devices, on_device(): lax.psum_scatter(jnp.dot(relaid_block, factor_full, precision=lax.Precisi...  26.9 us
    all_gather x1, blocking collectives, on_device(): factor_full = lax.all_gather(q_factor, 'row', axis=1, tiled=True)  16.7 us
    unnamed x1, blocking collectives  13.6 us
    all_to_all x1, starting transfers between devices, on_device(): lax.all_to_all(flat_pieces, ('row', 'col'), split_axis=0, concat_axis=0,...  7.45 us
    dot_general x1, matrix products, on_device(): jnp.dot(relaid_block, factor_full, precision=lax.Precision.HIGHEST, prefe...  3.99 us
    gather x1, local copies, waits for them, and re-layouts, on_device(): arranged = jnp.take(received, placement, axis=0)  3.56 us
    select_n x2, other arithmetic, on_device(): jnp.take(old_residual.reshape(row_count, group_rows, full_width), sending...  3.28 us
  transfers between devices with their start and end apart: 2, of which 2 were waited for; matrix products, arithmetic and copies ran while one was open for 3% of the time, Pallas kernels for 0%

commit v1 on v0

v1 whole, which is shorter than its diff:
```python
import functools

import jax
import jax.numpy as jnp
from jax import lax
from jax.experimental import pallas as pl
from jax.experimental.pallas import tpu as pltpu
from jax.sharding import PartitionSpec as P

epsilon = 1e-06
MESH = pl.DeviceIdType.MESH


def flip(x, bits):
    b = 1
    while b <= bits:
        if bits & b:
            x = x + b * (1 - 2 * lax.rem(lax.div(x, b), 2))
        b *= 2
    return x


def kernel(
    rows, cols, map_ref, old_ref, q_ref,
    out_ref, proj_ref, sums_ref,
    old, picked, recv, qbuf, qwide, part, squares, tail_out, tail_in,
    ids, inverse,
    in_sem, own_sem, send_sem, recv_sem, q_send, q_recv, q_own, t_send, t_recv,
):
    total = rows * cols
    my_row, my_col = lax.axis_index("row"), lax.axis_index("col")
    me = my_row * cols + my_col
    group = old.shape[1]
    width = recv.shape[2]
    rank_part = qbuf.shape[1]
    rank = rows * rank_part
    lanes = rows * rank

    fetch = pltpu.make_async_copy(old_ref, old, in_sem)
    fetch.start()
    q_fetch = pltpu.make_async_copy(q_ref, qbuf.at[my_row], q_own)
    q_fetch.start()

    barrier = pltpu.get_barrier_semaphore()
    for u in range(rows):
        for v in range(cols):
            if u or v:
                pl.semaphore_signal(
                    barrier, inc=1, device_id=(flip(my_row, u), flip(my_col, v)), device_id_type=MESH
                )

    fetch.wait()
    for k in range(rows):
        slot = 0
        for j in range(rows):
            slot = jnp.where(lax.div(map_ref[me, j], total) == k, j, slot)
        picked[k] = old[slot]
    q_fetch.wait()
    pl.semaphore_wait(barrier, total - 1)

    def piece(r, c):
        return picked.at[r, :, pl.ds(pl.multiple_of(c * width, width), width)]

    def move(u, v):
        r, c = flip(my_row, u), flip(my_col, v)
        return pltpu.make_async_remote_copy(
            src_ref=piece(r, c),
            dst_ref=recv.at[me],
            send_sem=send_sem.at[r * cols + c],
            recv_sem=recv_sem.at[me],
            device_id=(r, c),
            device_id_type=MESH,
        )

    def arrival(u, v):
        r, c = flip(my_row, u), flip(my_col, v)
        source = r * cols + c
        return pltpu.make_async_remote_copy(
            src_ref=piece(r, c),
            dst_ref=recv.at[source],
            send_sem=send_sem.at[source],
            recv_sem=recv_sem.at[source],
            device_id=(r, c),
            device_id_type=MESH,
        )

    def q_move(u, slot):
        return pltpu.make_async_remote_copy(
            src_ref=qbuf.at[my_row],
            dst_ref=qbuf.at[slot],
            send_sem=q_send.at[flip(my_row, u)],
            recv_sem=q_recv.at[slot],
            device_id=(flip(my_row, u), my_col),
            device_id_type=MESH,
        )

    far = [v for v in range(cols - 1, -1, -1) if v >= cols // 2]
    near = [v for v in range(cols - 1, -1, -1) if v < cols // 2]
    for v in far:
        for u in range(rows):
            move(u, v).start()
    for u in range(1, rows):
        q_move(u, my_row).start()
    for v in near:
        for u in range(rows):
            if u or v:
                move(u, v).start()
    own = pltpu.make_async_copy(piece(my_row, my_col), recv.at[me], own_sem)
    own.start()

    def read_ids(d, _):
        found = 0
        for j in range(rows):
            value = map_ref[d, j]
            found = jnp.where(lax.div(value, total) == my_row, value - my_row * total, found)
        ids[d] = found
        return 0

    lax.fori_loop(0, total, read_ids, 0)

    def invert(g, _):
        found = 0
        for d in range(total):
            found = jnp.where(ids[d] == g, d, found)
        inverse[g] = found
        return 0

    lax.fori_loop(0, total, invert, 0)

    for u in range(1, rows):
        q_move(u, flip(my_row, u)).wait_recv()
    for m in range(rows):
        for k in range(rows):
            qwide[pl.ds(m * rank + k * rank_part, rank_part), :] = qbuf[k]

    own.wait()
    for v in near[::-1] + far:
        for u in range(rows):
            if u or v:
                arrival(u, v).wait_recv()
        sources = [flip(my_row, u) * cols + flip(my_col, v) for u in range(rows)]
        block = jnp.concatenate([recv[s] for s in sources], axis=0)
        product = lax.dot_general(
            block,
            qwide[...],
            (((1,), (1,)), ((), ())),
            precision=lax.Precision.HIGHEST,
            preferred_element_type=jnp.float32,
        )
        row_sums = jnp.sum(block * block, axis=1, keepdims=True)
        for u in range(rows):
            part[sources[u]] = product[u * group:(u + 1) * group]
            squares[sources[u]] = jnp.broadcast_to(row_sums[u * group:(u + 1) * group], (group, 128))

    p_lane = lax.broadcasted_iota(jnp.int32, (group, lanes), 1)
    s_lane = lax.broadcasted_iota(jnp.int32, (group, 128), 1)
    for c in range(cols):
        p_tile = jnp.zeros((group, lanes), jnp.float32)
        s_tile = jnp.zeros((group, 128), jnp.float32)
        for m in range(rows):
            source = inverse[c * rows + m]
            p_tile = jnp.where(lax.div(p_lane, rank) == m, part[source], p_tile)
            s_tile = jnp.where(s_lane == m, squares[source], s_tile)
        tail_out[c, :, pl.ds(0, lanes)] = p_tile
        tail_out[c, :, pl.ds(lanes, 128)] = s_tile

    def tail(v, slot):
        c = flip(my_col, v)
        return pltpu.make_async_remote_copy(
            src_ref=tail_out.at[c],
            dst_ref=tail_in.at[slot],
            send_sem=t_send.at[c],
            recv_sem=t_recv.at[slot],
            device_id=(my_row, c),
            device_id_type=MESH,
        )

    for v in range(cols - 1, 0, -1):
        tail(v, my_col).start()

    for g in range(total):
        out_ref[g] = recv[inverse[g]]

    result = tail_out[my_col]
    for v in range(1, cols):
        c = flip(my_col, v)
        tail(v, c).wait_recv()
        result = result + tail_in[c]
    turned = result[:, :lanes].T
    for m in range(rows):
        proj_ref[:, pl.ds(m * group, group)] = turned[m * rank:(m + 1) * rank, :]
    sums_ref[...] = jnp.sqrt(result[:, lanes:] / (width * cols) + epsilon)

    for u in range(rows):
        for v in range(cols):
            if u or v:
                move(u, v).wait_send()
    for u in range(1, rows):
        q_move(u, my_row).wait_send()
    for v in range(1, cols):
        tail(v, my_col).wait_send()


def on_device(rows, cols, old_residual, group_map, q_factor):
    total = rows * cols
    height, full = old_residual.shape
    group = height // rows
    width = full // cols
    depth, rank_part = q_factor.shape
    rank = rank_part * rows
    lanes = rows * rank
    f32 = jnp.float32
    hbm = pl.BlockSpec(memory_space=pl.ANY)
    vmem = pl.BlockSpec(memory_space=pltpu.VMEM)
    dma = pltpu.SemaphoreType.DMA
    relaid, projection, norms = pl.pallas_call(
        functools.partial(kernel, rows, cols),
        out_shape=[
            jax.ShapeDtypeStruct((total, group, width), f32),
            jax.ShapeDtypeStruct((rank, rows * group), f32),
            jax.ShapeDtypeStruct((group, 128), f32),
        ],
        in_specs=[pl.BlockSpec(memory_space=pltpu.SMEM), hbm, hbm],
        out_specs=[vmem, vmem, vmem],
        scratch_shapes=[
            pltpu.VMEM((rows, group, full), f32),
            pltpu.VMEM((rows, group, full), f32),
            pltpu.VMEM((total, group, width), f32),
            pltpu.VMEM((rows, rank_part, depth), f32),
            pltpu.VMEM((lanes, depth), f32),
            pltpu.VMEM((total, group, lanes), f32),
            pltpu.VMEM((total, group, 128), f32),
            pltpu.VMEM((cols, group, lanes + 128), f32),
            pltpu.VMEM((cols, group, lanes + 128), f32),
            pltpu.SMEM((total,), jnp.int32),
            pltpu.SMEM((total,), jnp.int32),
            dma, dma,
            dma((total,)), dma((total,)),
            dma((rows,)), dma((rows,)), dma,
            dma((cols,)), dma((cols,)),
        ],
        compiler_params=pltpu.CompilerParams(
            collective_id=0, has_side_effects=True, vmem_limit_bytes=50 * 1024 * 1024
        ),
    )(group_map, old_residual.reshape(rows, group, full), q_factor.T)
    return (
        relaid.reshape(total * group, width),
        projection,
        norms[:, :rows].T.reshape(rows * group),
    )


def solution(mesh):
    rows, cols = mesh.shape["row"], mesh.shape["col"]
    placed = (P(("row", "col"), None), P(), P("col", "row"))
    return jax.shard_map(
        functools.partial(on_device, rows, cols),
        mesh=mesh,
        in_specs=placed,
        out_specs=(P("row", "col"), P(None, ("row", "col")), P(("row", "col"))),
        check_vma=False,
    )
```

time: 134 us -> 67.1 us (0.50)
  Pallas kernels: 0 us -> 62.1 us
  waiting for transfers between devices: 56.4 us -> 0 us
  blocking collectives: 30.3 us -> 0 us
  between operations: 14.8 us -> 0.65 us
  other arithmetic: 11.9 us -> 0 us
  starting transfers between devices: 7.5 us -> 0 us
  local copies, waits for them, and re-layouts: 8.86 us -> 4.21 us
  matrix products: 3.99 us -> 0 us
    pallas_call x0 -> x1, Pallas kernels: none -> 62.1 us  [on_device(): pl.pallas_call(functools.partial(kernel, rows, cols), out_shape=[jax.Shap...]
    all_to_all x1 -> x0, waiting for transfers between devices: 29.5 us -> none  [on_device(): lax.all_to_all(flat_pieces, ('row', 'col'), split_axis=0, concat_axis=0,...]
    reduce_scatter x1 -> x0, waiting for transfers between devices: 26.9 us -> none  [on_device(): lax.psum_scatter(jnp.dot(relaid_block, factor_full, precision=lax.Precisi...]
    all_gather x1 -> x0, blocking collectives: 16.7 us -> none  [on_device(): factor_full = lax.all_gather(q_factor, 'row', axis=1, tiled=True)]
    unnamed x1 -> x0, blocking collectives: 13.6 us -> none
    all_to_all x1 -> x0, starting transfers between devices: 7.45 us -> none  [on_device(): lax.all_to_all(flat_pieces, ('row', 'col'), split_axis=0, concat_axis=0,...]
    select_n x4 -> x0, other arithmetic: 6.4 us -> none  [the longest x2 3.28 us: on_device(): jnp.take(old_residual.reshape(row_count, group_rows, full_width), sending...]
    gather x2 -> x0, local copies, waits for them, and re-layouts: 5.56 us -> none  [the longest x1 3.56 us: on_device(): arranged = jnp.take(received, placement, axis=0)]
  transfers between devices with their start and end apart: 2 -> 0, of which waited for: 2 -> 0; matrix products, arithmetic and copies ran while one was open for 3% -> 0% of each run, Pallas kernels for 0% -> 0%
where the time goes in v1:
time: 67.1 us; the launch traced here: 66.9 us
  Pallas kernels  62.1 us (93%)
  local copies, waits for them, and re-layouts  4.21 us (6%)
    pallas_call x1, Pallas kernels, on_device(): pl.pallas_call(functools.partial(kernel, rows, cols), out_shape=[jax.Shap...  62.1 us
    unnamed x5, local copies, waits for them, and re-layouts  3.53 us

profile of v1, /device:TPU:0, one launch (start us, length us, event | category | flops | bytes accessed | tf_op | source)
XLA Modules:
  0.0 66.9 jit_solution(735788456904640437)
XLA Ops:
  0.6 0.8 %copy.6.map_ref = s32[32,4]{1,0:T(8,128)S(1)} copy(s32[32,4]{0,1:T(4,128)} %param.4) | data formatting | bytes 1024 | tf_op args[1]
  1.4 0.0 copy-start
  1.4 0.8 %copy-done = f32[2048,8]{0,1:T(8,128)S(1)} copy-done((f32[2048,8]{0,1:T(8,128)S(1)}, f32[2048,8]{0,1:T(8,128)}, u32[]{:S(2)}) %copy-start) | copy-done | bytes 65560
  2.2 62.1 %shard_map.58 = (f32[32,8,2048]{2,1,0:T(8,128)S(1)}, f32[32,32]{1,0:T(8,128)S(1)}, f32[8,128]{1,0:T(8,128)S(1)}) custom-call(s32[32,4]{1,0:T(8,128)S(1)} %copy.6.map_ref, f32[4,8,16384]{2,1,0:T(8,128)} %bitcast.7, f32[8,2048]{1,0:T(8,128)S(1)} %bitcast.6), custom_call_target="tpu_custom_call" | custom-call | tf_op jit(solution)/shard_map/pallas_call | solution.py:216
  64.3 0.1 copy.7
  64.4 0.6 reshape.17
  65.0 1.3 %copy.10 = f32[256,2048]{1,0:T(8,128)} copy(f32[256,2048]{1,0:T(8,128)S(1)} %bitcast.5) | data formatting | bytes 4194304
  66.3 0.6 copy.11
  (1 shorter events, 0.0 us)
Async XLA Ops:
  1.4 0.8 %copy-start = (f32[2048,8]{0,1:T(8,128)S(1)}, f32[2048,8]{0,1:T(8,128)}, u32[]{:S(2)}) copy-start(f32[2048,8]{0,1:T(8,128)} %param.5) | copy-start | bytes 196612

commit v2 on v1

--- a/solution.py
+++ b/solution.py
@@ -22,25 +22,20 @@
 
 def kernel(
     rows, cols, map_ref, old_ref, q_ref,
-    out_ref, proj_ref, sums_ref,
-    old, picked, recv, qbuf, qwide, part, squares, tail_out, tail_in,
+    recv, proj_ref, norm_ref,
+    old, picked, qbuf, part, squares, tail_out, tail_in,
     ids, inverse,
-    in_sem, own_sem, send_sem, recv_sem, q_send, q_recv, q_own, t_send, t_recv,
+    in_sems, own_sem, send_sem, recv_sem, q_send, q_recv, q_own, t_send, t_recv,
 ):
     total = rows * cols
     my_row, my_col = lax.axis_index("row"), lax.axis_index("col")
     me = my_row * cols + my_col
-    group = old.shape[1]
+    group = recv.shape[1]
     width = recv.shape[2]
     rank_part = qbuf.shape[1]
     rank = rows * rank_part
     lanes = rows * rank
 
-    fetch = pltpu.make_async_copy(old_ref, old, in_sem)
-    fetch.start()
-    q_fetch = pltpu.make_async_copy(q_ref, qbuf.at[my_row], q_own)
-    q_fetch.start()
-
     barrier = pltpu.get_barrier_semaphore()
     for u in range(rows):
         for v in range(cols):
@@ -49,22 +44,36 @@
                     barrier, inc=1, device_id=(flip(my_row, u), flip(my_col, v)), device_id_type=MESH
                 )
 
-    fetch.wait()
-    for k in range(rows):
+    order = [v for v in range(cols - 1, -1, -1)]
+    far, near = order[:cols // 2], order[cols // 2:]
+
+    def fetch(v):
+        start = pl.multiple_of(flip(my_col, v) * width, width)
+        return pltpu.make_async_copy(old_ref.at[:, :, pl.ds(start, width)], old[v], in_sems.at[v])
+
+    for v in order:
+        fetch(v).start()
+    q_fetch = pltpu.make_async_copy(q_ref, qbuf.at[my_row], q_own)
+    q_fetch.start()
+
+    def slot_of(r):
         slot = 0
         for j in range(rows):
-            slot = jnp.where(lax.div(map_ref[me, j], total) == k, j, slot)
-        picked[k] = old[slot]
-    q_fetch.wait()
-    pl.semaphore_wait(barrier, total - 1)
-
-    def piece(r, c):
-        return picked.at[r, :, pl.ds(pl.multiple_of(c * width, width), width)]
+            slot = jnp.where(lax.div(map_ref[j, me], total) == r, j, slot)
+        return slot
+
+    partners = [flip(my_row, u) for u in range(rows)]
+    slots = [slot_of(r) for r in partners]
+
+    def pick(v):
+        fetch(v).wait()
+        for u in range(rows):
+            picked[v, u] = old[v][slots[u]]
 
     def move(u, v):
         r, c = flip(my_row, u), flip(my_col, v)
         return pltpu.make_async_remote_copy(
-            src_ref=piece(r, c),
+            src_ref=picked.at[v, u],
             dst_ref=recv.at[me],
             send_sem=send_sem.at[r * cols + c],
             recv_sem=recv_sem.at[me],
@@ -76,7 +85,7 @@
         r, c = flip(my_row, u), flip(my_col, v)
         source = r * cols + c
         return pltpu.make_async_remote_copy(
-            src_ref=piece(r, c),
+            src_ref=picked.at[v, u],
             dst_ref=recv.at[source],
             send_sem=send_sem.at[source],
             recv_sem=recv_sem.at[source],
@@ -94,24 +103,28 @@
             device_id_type=MESH,
         )
 
-    far = [v for v in range(cols - 1, -1, -1) if v >= cols // 2]
-    near = [v for v in range(cols - 1, -1, -1) if v < cols // 2]
+    pick(far[0])
+    pl.semaphore_wait(barrier, total - 1)
     for v in far:
+        if v != far[0]:
+            pick(v)
         for u in range(rows):
             move(u, v).start()
+    q_fetch.wait()
     for u in range(1, rows):
         q_move(u, my_row).start()
     for v in near:
+        pick(v)
         for u in range(rows):
             if u or v:
                 move(u, v).start()
-    own = pltpu.make_async_copy(piece(my_row, my_col), recv.at[me], own_sem)
+    own = pltpu.make_async_copy(picked.at[0, 0], recv.at[me], own_sem)
     own.start()
 
     def read_ids(d, _):
         found = 0
         for j in range(rows):
-            value = map_ref[d, j]
+            value = map_ref[j, d]
             found = jnp.where(lax.div(value, total) == my_row, value - my_row * total, found)
         ids[d] = found
         return 0
@@ -129,10 +142,7 @@
 
     for u in range(1, rows):
         q_move(u, flip(my_row, u)).wait_recv()
-    for m in range(rows):
-        for k in range(rows):
-            qwide[pl.ds(m * rank + k * rank_part, rank_part), :] = qbuf[k]
-
+    factor = qbuf[...].reshape(rank, width)
     own.wait()
     for v in near[::-1] + far:
         for u in range(rows):
@@ -142,14 +152,15 @@
         block = jnp.concatenate([recv[s] for s in sources], axis=0)
         product = lax.dot_general(
             block,
-            qwide[...],
+            factor,
             (((1,), (1,)), ((), ())),
             precision=lax.Precision.HIGHEST,
             preferred_element_type=jnp.float32,
         )
         row_sums = jnp.sum(block * block, axis=1, keepdims=True)
         for u in range(rows):
-            part[sources[u]] = product[u * group:(u + 1) * group]
+            own_rows = product[u * group:(u + 1) * group]
+            part[sources[u]] = jnp.concatenate([own_rows] * rows, axis=1)
             squares[sources[u]] = jnp.broadcast_to(row_sums[u * group:(u + 1) * group], (group, 128))
 
     p_lane = lax.broadcasted_iota(jnp.int32, (group, lanes), 1)
@@ -178,9 +189,6 @@
     for v in range(cols - 1, 0, -1):
         tail(v, my_col).start()
 
-    for g in range(total):
-        out_ref[g] = recv[inverse[g]]
-
     result = tail_out[my_col]
     for v in range(1, cols):
         c = flip(my_col, v)
@@ -189,7 +197,9 @@
     turned = result[:, :lanes].T
     for m in range(rows):
         proj_ref[:, pl.ds(m * group, group)] = turned[m * rank:(m + 1) * rank, :]
-    sums_ref[...] = jnp.sqrt(result[:, lanes:] / (width * cols) + epsilon)
+    norms = jnp.sqrt(result[:, lanes:] / (width * cols) + epsilon).T
+    for m in range(rows):
+        norm_ref[:, pl.ds(m * group, group)] = norms[m:m + 1, :]
 
     for u in range(rows):
         for v in range(cols):
@@ -199,6 +209,27 @@
         q_move(u, my_row).wait_send()
     for v in range(1, cols):
         tail(v, my_col).wait_send()
+
+
+def place(rows, cols, map_ref, recv, proj_in, norm_in, out_ref, proj_ref, norm_ref, sems, small_sems):
+    total = rows * cols
+    my_row = lax.axis_index("row")
+    smalls = [
+        pltpu.make_async_copy(proj_in, proj_ref, small_sems.at[0]),
+        pltpu.make_async_copy(norm_in, norm_ref, small_sems.at[1]),
+    ]
+    for d in range(total):
+        where = 0
+        for j in range(rows):
+            value = map_ref[j, d]
+            where = jnp.where(lax.div(value, total) == my_row, value - my_row * total, where)
+        pltpu.make_async_copy(recv.at[d], out_ref.at[where], sems.at[d]).start()
+    for small in smalls:
+        small.start()
+    for d in range(total):
+        pltpu.make_async_copy(recv.at[d], out_ref.at[d], sems.at[d]).wait()
+    for small in smalls:
+        small.wait()
 
 
 def on_device(rows, cols, old_residual, group_map, q_factor):
@@ -210,31 +241,32 @@
     rank = rank_part * rows
     lanes = rows * rank
     f32 = jnp.float32
-    hbm = pl.BlockSpec(memory_space=pl.ANY)
+    hbm = pl.BlockSpec(memory_space=pltpu.HBM)
     vmem = pl.BlockSpec(memory_space=pltpu.VMEM)
     dma = pltpu.SemaphoreType.DMA
-    relaid, projection, norms = pl.pallas_call(
+    map_turned = group_map.T
+    shapes = [
+        jax.ShapeDtypeStruct((total, group, width), f32),
+        jax.ShapeDtypeStruct((rank, rows * group), f32),
+        jax.ShapeDtypeStruct((1, rows * group), f32),
+    ]
+    smem = pl.BlockSpec(memory_space=pltpu.SMEM)
+    arrived = pl.pallas_call(
         functools.partial(kernel, rows, cols),
-        out_shape=[
-            jax.ShapeDtypeStruct((total, group, width), f32),
-            jax.ShapeDtypeStruct((rank, rows * group), f32),
-            jax.ShapeDtypeStruct((group, 128), f32),
-        ],
-        in_specs=[pl.BlockSpec(memory_space=pltpu.SMEM), hbm, hbm],
+        out_shape=shapes,
+        in_specs=[smem, hbm, hbm],
         out_specs=[vmem, vmem, vmem],
         scratch_shapes=[
-            pltpu.VMEM((rows, group, full), f32),
-            pltpu.VMEM((rows, group, full), f32),
-            pltpu.VMEM((total, group, width), f32),
+            [pltpu.VMEM((rows, group, width), f32)] * cols,
+            pltpu.VMEM((cols, rows, group, width), f32),
             pltpu.VMEM((rows, rank_part, depth), f32),
-            pltpu.VMEM((lanes, depth), f32),
             pltpu.VMEM((total, group, lanes), f32),
             pltpu.VMEM((total, group, 128), f32),
             pltpu.VMEM((cols, group, lanes + 128), f32),
             pltpu.VMEM((cols, group, lanes + 128), f32),
             pltpu.SMEM((total,), jnp.int32),
             pltpu.SMEM((total,), jnp.int32),
-            dma, dma,
+            dma((cols,)), dma,
             dma((total,)), dma((total,)),
             dma((rows,)), dma((rows,)), dma,
             dma((cols,)), dma((cols,)),
@@ -242,12 +274,16 @@
         compiler_params=pltpu.CompilerParams(
             collective_id=0, has_side_effects=True, vmem_limit_bytes=50 * 1024 * 1024
         ),
-    )(group_map, old_residual.reshape(rows, group, full), q_factor.T)
-    return (
-        relaid.reshape(total * group, width),
-        projection,
-        norms[:, :rows].T.reshape(rows * group),
-    )
+    )(map_turned, old_residual.reshape(rows, group, full), q_factor.T)
+    relaid, projection, norms = pl.pallas_call(
+        functools.partial(place, rows, cols),
+        out_shape=shapes,
+        in_specs=[smem, vmem, vmem, vmem],
+        out_specs=[hbm, hbm, hbm],
+        scratch_shapes=[dma((total,)), dma((2,))],
+        compiler_params=pltpu.CompilerParams(vmem_limit_bytes=8 * total * group * width),
+    )(map_turned, *arrived)
+    return relaid.reshape(total * group, width), projection, norms.reshape(rows * group)
 
 
 def solution(mesh):

time: 67.1 us -> 65.6 us (0.978)
  local copies, waits for them, and re-layouts: 4.21 us -> 1.51 us
  Pallas kernels: 62.1 us -> 63.2 us
    unnamed x5 -> x4, local copies, waits for them, and re-layouts: 3.53 us -> 1.51 us
    pallas_call x1 -> x2, Pallas kernels: 62.1 us -> 63.2 us  [the longest x1 61 us: on_device(): pl.pallas_call(functools.partial(kernel, rows, cols), out_shape=shapes, i...]
where the time goes in v2:
time: 65.6 us; the launch traced here: 65.4 us
  Pallas kernels  63.2 us (96%)
  local copies, waits for them, and re-layouts  1.51 us (2%)
    pallas_call x1, Pallas kernels, on_device(): pl.pallas_call(functools.partial(kernel, rows, cols), out_shape=shapes, i...  61 us
    pallas_call x1, Pallas kernels, on_device(): pl.pallas_call(functools.partial(place, rows, cols), out_shape=shapes, in...  2.18 us
    unnamed x4, local copies, waits for them, and re-layouts  1.51 us

profile of v2, /device:TPU:0, one launch (start us, length us, event | category | flops | bytes accessed | tf_op | source)
XLA Modules:
  0.0 65.4 jit_solution(8249235661167483222)
XLA Ops:
  0.6 0.0 copy-start
  0.6 0.8 %copy-done = f32[2048,8]{0,1:T(8,128)S(1)} copy-done((f32[2048,8]{0,1:T(8,128)S(1)}, f32[2048,8]{0,1:T(8,128)}, u32[]{:S(2)}) %copy-start) | copy-done | bytes 65560
  1.5 0.0 copy-start.1
  1.5 0.7 %copy-done.1 = s32[32,4]{0,1:T(4,128)S(1)} copy-done((s32[32,4]{0,1:T(4,128)S(1)}, s32[32,4]{0,1:T(4,128)}, u32[]{:S(2)}) %copy-start.1) | copy-done | bytes 536
  2.2 61.0 %shard_map.58 = (f32[32,8,2048]{2,1,0:T(8,128)S(1)}, f32[32,32]{1,0:T(8,128)S(1)}, f32[1,32]{1,0:T(1,128)S(1)}) custom-call(s32[4,32]{1,0:T(4,128)S(1)} %bitcast.6, f32[4,8,16384]{2,1,0:T(8,128)} %bitcast.8, f32[8,2048]{1,0:T(8,128)S(1)} %bitcast.5), custom_call_target="tpu_custom_call" | custom-call | tf_op jit(solution)/shard_map/pallas_call | solution.py:254
  63.2 2.2 %shard_map.59 = (f32[32,8,2048]{2,1,0:T(8,128)}, f32[32,32]{1,0:T(8,128)}, f32[1,32]{1,0:T(1,128)}) custom-call(s32[4,32]{1,0:T(4,128)S(1)} %bitcast.7, f32[32,8,2048]{2,1,0:T(8,128)S(1)} %get-tuple-element.9.recv, f32[32,32]{1,0:T(8,128)S(1)} %get-tuple-element.10.proj_in, f32[1,32]{1,0:T(1,128)S(1)} %get-tuple-element.11.norm_in), custom_call_target="tpu_custom_call" | custom-call | tf_op jit(solution)/shard_map/pallas_call | solution.py:278
Async XLA Ops:
  0.6 0.8 %copy-start = (f32[2048,8]{0,1:T(8,128)S(1)}, f32[2048,8]{0,1:T(8,128)}, u32[]{:S(2)}) copy-start(f32[2048,8]{0,1:T(8,128)} %param.5) | copy-start | bytes 196612
  1.5 0.7 %copy-start.1 = (s32[32,4]{0,1:T(4,128)S(1)}, s32[32,4]{0,1:T(4,128)}, u32[]{:S(2)}) copy-start(s32[32,4]{0,1:T(4,128)} %param.4) | copy-start | bytes 1540

commit v3 on v2

--- a/solution.py
+++ b/solution.py
@@ -161,19 +161,20 @@
         for u in range(rows):
             own_rows = product[u * group:(u + 1) * group]
             part[sources[u]] = jnp.concatenate([own_rows] * rows, axis=1)
-            squares[sources[u]] = jnp.broadcast_to(row_sums[u * group:(u + 1) * group], (group, 128))
+            squares[sources[u]] = jnp.broadcast_to(row_sums[u * group:(u + 1) * group], (group, lanes))
 
     p_lane = lax.broadcasted_iota(jnp.int32, (group, lanes), 1)
-    s_lane = lax.broadcasted_iota(jnp.int32, (group, 128), 1)
+    s_lane = lax.broadcasted_iota(jnp.int32, (group, lanes), 1)
+    s_row = lax.broadcasted_iota(jnp.int32, (group, lanes), 0)
     for c in range(cols):
         p_tile = jnp.zeros((group, lanes), jnp.float32)
-        s_tile = jnp.zeros((group, 128), jnp.float32)
+        s_tile = jnp.zeros((group, lanes), jnp.float32)
         for m in range(rows):
             source = inverse[c * rows + m]
             p_tile = jnp.where(lax.div(p_lane, rank) == m, part[source], p_tile)
-            s_tile = jnp.where(s_lane == m, squares[source], s_tile)
-        tail_out[c, :, pl.ds(0, lanes)] = p_tile
-        tail_out[c, :, pl.ds(lanes, 128)] = s_tile
+            s_tile = jnp.where(s_lane == m * group + s_row, squares[source], s_tile)
+        tail_out[c, pl.ds(0, group), :] = p_tile
+        tail_out[c, pl.ds(group, 1), :] = jnp.sum(s_tile, axis=0, keepdims=True)
 
     def tail(v, slot):
         c = flip(my_col, v)
@@ -194,12 +195,10 @@
         c = flip(my_col, v)
         tail(v, c).wait_recv()
         result = result + tail_in[c]
-    turned = result[:, :lanes].T
+    turned = result[:group].T
     for m in range(rows):
         proj_ref[:, pl.ds(m * group, group)] = turned[m * rank:(m + 1) * rank, :]
-    norms = jnp.sqrt(result[:, lanes:] / (width * cols) + epsilon).T
-    for m in range(rows):
-        norm_ref[:, pl.ds(m * group, group)] = norms[m:m + 1, :]
+    norm_ref[...] = jnp.sqrt(result[group:, :rows * group] / (width * cols) + epsilon)
 
     for u in range(rows):
         for v in range(cols):
@@ -261,9 +260,9 @@
             pltpu.VMEM((cols, rows, group, width), f32),
             pltpu.VMEM((rows, rank_part, depth), f32),
             pltpu.VMEM((total, group, lanes), f32),
-            pltpu.VMEM((total, group, 128), f32),
-            pltpu.VMEM((cols, group, lanes + 128), f32),
-            pltpu.VMEM((cols, group, lanes + 128), f32),
+            pltpu.VMEM((total, group, lanes), f32),
+            pltpu.VMEM((cols, group + 1, lanes), f32),
+            pltpu.VMEM((cols, group + 1, lanes), f32),
             pltpu.SMEM((total,), jnp.int32),
             pltpu.SMEM((total,), jnp.int32),
             dma((cols,)), dma,
@@ -274,7 +273,11 @@
         compiler_params=pltpu.CompilerParams(
             collective_id=0, has_side_effects=True, vmem_limit_bytes=50 * 1024 * 1024
         ),
-    )(map_turned, old_residual.reshape(rows, group, full), q_factor.T)
+    )(
+        pltpu.with_memory_space_constraint(map_turned, pltpu.HBM),
+        old_residual.reshape(rows, group, full),
+        pltpu.with_memory_space_constraint(q_factor.T, pltpu.HBM),
+    )
     relaid, projection, norms = pl.pallas_call(
         functools.partial(place, rows, cols),
         out_shape=shapes,

time: 65.6 us -> 64 us (0.976)
  local copies, waits for them, and re-layouts: 1.51 us -> 0.01 us
    unnamed x4 -> x2, local copies, waits for them, and re-layouts: 1.51 us -> 0.01 us
where the time goes in v3:
time: 64 us; the launch traced here: 63.8 us
  Pallas kernels  63.1 us (99%)
  between operations  0.65 us (1%)
    pallas_call x1, Pallas kernels, on_device(): pl.pallas_call(functools.partial(kernel, rows, cols), out_shape=shapes, i...  61 us
    pallas_call x1, Pallas kernels, on_device(): pl.pallas_call(functools.partial(place, rows, cols), out_shape=shapes, in...  2.18 us

profile of v3, /device:TPU:0, one launch (start us, length us, event | category | flops | bytes accessed | tf_op | source)
XLA Modules:
  0.0 63.8 jit_solution(15280262228965276852)
XLA Ops:
  0.6 0.0 copy-start
  0.6 61.0 %shard_map.58 = (f32[32,8,2048]{2,1,0:T(8,128)S(1)}, f32[32,32]{1,0:T(8,128)S(1)}, f32[1,32]{1,0:T(1,128)S(1)}) custom-call(s32[4,32]{1,0:T(4,128)} %bitcast.5, f32[4,8,16384]{2,1,0:T(8,128)} %bitcast.7, f32[8,2048]{1,0:T(8,128)} %bitcast.8), custom_call_target="tpu_custom_call" | custom-call | tf_op jit(solution)/shard_map/pallas_call | solution.py:253
  61.6 0.0 copy-done
  61.6 2.2 %shard_map.59 = (f32[32,8,2048]{2,1,0:T(8,128)}, f32[32,32]{1,0:T(8,128)}, f32[1,32]{1,0:T(1,128)}) custom-call(s32[4,32]{1,0:T(4,128)S(1)} %bitcast.6, f32[32,8,2048]{2,1,0:T(8,128)S(1)} %get-tuple-element.9.recv, f32[32,32]{1,0:T(8,128)S(1)} %get-tuple-element.10.proj_in, f32[1,32]{1,0:T(1,128)S(1)} %get-tuple-element.11.norm_in), custom_call_target="tpu_custom_call" | custom-call | tf_op jit(solution)/shard_map/pallas_call | solution.py:281
Async XLA Ops:
  0.6 61.0 %copy-start = (s32[32,4]{0,1:T(4,128)S(1)}, s32[32,4]{0,1:T(4,128)}, u32[]{:S(2)}) copy-start(s32[32,4]{0,1:T(4,128)} %param.4) | copy-start | bytes 1540
